TPU v7x, 32 devices: a whole 2x2x4 slice. The times are simulated.
32 devices in a mesh: rep: 4 (over x, y), dp: 8 (over z, core).
Axes of the slice: x: 2, y: 2, z: 4, core: 2. Of those that a mesh axis runs over, the one named last changes fastest.
Arguments:
- x: bfloat16 [32, 4096, 896], P(('rep', 'dp')), parts along dimension 0
- dy: bfloat16 [32, 4096, 896], P(('rep', 'dp')), parts along dimension 0
- w_gate: bfloat16 [2, 896, 2560], P(None, 'dp')
- w_up: bfloat16 [2, 896, 2560], P(None, 'dp')
- w_down: bfloat16 [2, 2560, 896], P(None, 'dp')
Outputs:
- output 1: bfloat16 [32, 4096, 896], P(('rep', 'dp')), parts along dimension 0
- output 2: bfloat16 [8, 896, 2560], P('rep', 'dp'), parts along dimension 0
- output 3: bfloat16 [8, 896, 2560], P('rep', 'dp'), parts along dimension 0
- output 4: bfloat16 [8, 2560, 896], P('rep', 'dp'), parts along dimension 0
There are 4 independent parts. A program takes and returns all parts, laid end to end along the dimension named above; an argument that names none is the same for every part.
All inputs are finite; a program needn't handle non-finite values.
Results may differ from a plain program's by a relative error of at most 0.018.
Values are sent between devices in bfloat16 or wider.
A program may use at most 2 GiB of HBM per device.

v0:
```python
import jax
import jax.numpy as jnp
from jax import lax

NAMES = ("w_gate", "w_up", "w_down")


def matmul(a, w):
    return jnp.dot(a, w, preferred_element_type=jnp.float32).astype(jnp.bfloat16)


def normed(h):
    wide = h.astype(jnp.float32)
    scale = lax.rsqrt(jnp.mean(wide**2, -1, keepdims=True) + 1e-6)
    return (wide * scale).astype(jnp.bfloat16)


def layer(h, w):
    a = normed(h)
    gate = jnp.dot(a, w["w_gate"], preferred_element_type=jnp.float32)
    up = jnp.dot(a, w["w_up"], preferred_element_type=jnp.float32)
    return h + matmul((jax.nn.silu(gate) * up).astype(jnp.bfloat16), w["w_down"])


def stack(weights, h):
    for number in range(weights["w_gate"].shape[0]):
        h = layer(h, {name: w[number] for name, w in weights.items()})
    return h


def solution(mesh):
    groups = mesh.shape["rep"]

    def step(x, dy, *weights):
        shape = x.shape
        x, dy = (t.reshape(groups, -1, *t.shape[1:]) for t in (x, dy))

        def of_a_group(x, dy):
            _, back = jax.vjp(stack, dict(zip(NAMES, weights, strict=True)), x)
            by_weights, by_x = back(dy)
            return (by_x, *(by_weights[name] for name in NAMES))

        by_x, *by_weights = jax.vmap(of_a_group)(x, dy)
        return (by_x.reshape(shape), *(t.reshape(-1, *t.shape[2:]) for t in by_weights))

    return step
```

profile of v0, /device:TPU:0, one launch (start us, length us, event | category | flops | bytes accessed | tf_op | source)
XLA Modules:
  0.0 1394.4 jit_solution(1748919580744893650)
XLA Ops:
  62.4 29.4 %fusion.212 = f32[4096,2560]{1,0:T(8,128)} fusion(bf16[1,896,2560]{2,1,0:T(8,128)(2,1)} %all-gather.30.cloned.1.call-done, bf16[1,4096,896]{2,1,0:T(8,128)(2,1)} %param.13, f32[4096]{0:T(1024)S(1)} %get-tuple-element.267), kind=kOutput, calls=%fused_computation.252 | convolution fusion | flops 18801491968 | bytes 53886976 | tf_op jit(solution)/vmap(jvp())/dot_general | solution.py:20
  91.8 21.0 %all-gather.32.cloned.1.call-done = bf16[1,896,2560]{2,1,0:T(8,128)(2,1)} async-done(((bf16[1,112,2560]{2,1,0:T(8,128)(2,1)}), bf16[1,896,2560]{2,1,0:T(8,128)(2,1)}) %all-gather.32.cloned.1.call-update) | async-done | bytes 4587536 | tf_op jit(solution)/vmap(jvp())/squeeze | solution.py:27
  112.8 46.1 %fusion.168 = (bf16[1,1,4096,2560]{3,2,1,0:T(8,128)(2,1)}, f32[4096,2560]{1,0:T(8,128)}) fusion(f32[4096,2560]{1,0:T(8,128)} %fusion.212, bf16[1,896,2560]{2,1,0:T(8,128)(2,1)} %all-gather.32.cloned.1.call-done, bf16[1,4096,896]{2,1,0:T(8,128)(2,1)} %param.13, f32[4096]{0:T(1024)S(1)} %get-tuple-element.267), kind=kOutput, calls=%fused_computation.195 | convolution fusion | flops 18864406528 | bytes 116801536 | tf_op jit(solution)/vmap(jvp())/dot_general | solution.py:21
  163.2 26.0 %fusion.182 = (f32[4096]{0:T(1024)S(1)}, bf16[1,1,4096,896]{2,3,1,0:T(8,128)(2,1)S(1)}) fusion(bf16[1,2560,896]{2,1,0:T(8,128)(2,1)} %all-gather.34.cloned.1.call-done, bf16[1,1,4096,2560]{3,2,1,0:T(8,128)(2,1)} %get-tuple-element.268, bf16[1,4096,896]{1,2,0:T(8,128)(2,1)} %copy.1), kind=kOutput, calls=%fused_computation.225 | convolution fusion | flops 18808827904 | bytes 40255488 | tf_op jit(solution)/vmap(jvp())/dot_general | solution.py:9
  196.9 16.6 %all-gather.36.cloned.1.call-done = bf16[1,896,2560]{2,1,0:T(8,128)(2,1)} async-done(((bf16[1,112,2560]{2,1,0:T(8,128)(2,1)}), bf16[1,896,2560]{2,1,0:T(8,128)(2,1)}) %all-gather.36.cloned.1.call-update) | async-done | bytes 4587536 | tf_op jit(solution)/vmap(jvp())/squeeze | solution.py:27
  213.5 29.6 %fusion.193 = f32[4096,2560]{1,0:T(8,128)} fusion(bf16[1,1,4096,896]{2,3,1,0:T(8,128)(2,1)} %fusion.183, bf16[1,896,2560]{2,1,0:T(8,128)(2,1)} %all-gather.36.cloned.1.call-done), kind=kOutput, calls=%fused_computation.236 | convolution fusion | flops 18790481920 | bytes 53870592 | tf_op jit(solution)/vmap(jvp())/dot_general | solution.py:20
  243.0 20.7 %all-gather.40.cloned.1.call-done = bf16[1,896,2560]{2,1,0:T(8,128)(2,1)} async-done(((bf16[1,112,2560]{2,1,0:T(8,128)(2,1)}), bf16[1,896,2560]{2,1,0:T(8,128)(2,1)}) %all-gather.40.cloned.1.call-update) | async-done | bytes 4587536 | tf_op jit(solution)/vmap(jvp())/squeeze | solution.py:27
  263.7 46.3 %fusion.162 = (bf16[1,1,4096,2560]{3,2,1,0:T(8,128)(2,1)}, f32[4096,2560]{1,0:T(8,128)}) fusion(f32[4096,2560]{1,0:T(8,128)} %fusion.193, bf16[1,896,2560]{2,1,0:T(8,128)(2,1)} %all-gather.40.cloned.1.call-done, bf16[1,1,4096,896]{2,3,1,0:T(8,128)(2,1)} %fusion.183), kind=kOutput, calls=%fused_computation.185 | convolution fusion | flops 18853396480 | bytes 116785152 | tf_op jit(solution)/vmap(jvp())/dot_general | solution.py:21
  310.0 26.4 %copy.4 = bf16[1,1,4096,2560]{2,3,1,0:T(8,128)(2,1)} copy(bf16[1,1,4096,2560]{3,2,1,0:T(8,128)(2,1)} %get-tuple-element.268) | data formatting | bytes 41943040
  336.4 26.7 %copy.2 = bf16[1,1,4096,2560]{2,3,1,0:T(8,128)(2,1)} copy(bf16[1,1,4096,2560]{3,2,1,0:T(8,128)(2,1)} %get-tuple-element.275) | data formatting | bytes 41943040
  363.1 116.4 %while.16 = (bf16[1,1,4096,2560]{2,3,1,0:T(8,128)(2,1)}, bf16[1,1,4096,896]{3,2,1,0:T(8,128)(2,1)}, f32[1,320,896]{2,1,0:T(8,128)S(1)}, f32[1,320,896]{2,1,0:T(8...) while((bf16[1,1,4096,2560]{2,3,1,0:T(8,128)(2,1)}, ...), condition=%wide.windowed_dot_general_cond_rs.4.clone, body=%wide.windowed_dot_general_body_rs.4.clone.sunk | while | flops 9417932800 | bytes 160826096 | solution.py:9
  406.1 14.6 %collective-permute-done.18 = f32[1,320,896]{2,1,0:T(8,128)S(1)} collective-permute-done((f32[1,320,896]{2,1,0:T(8,128)S(1)}, f32[1,320,896]{2,1,0:T(8,128)S(1)}, u32[]{:S(2)}, u32[]{:S(2)}) %collective-permute-start.18) | collective-permute-done | bytes 1146912 | tf_op jit(solution)/vmap(transpose(jvp()))/dot_general | solution.py:9
  480.9 55.3 %convert_multiply_fusion.3 = (bf16[1,1,4096,2560]{3,2,1,0:T(8,128)(2,1)}, bf16[1,1,4096,2560]{3,2,1,0:T(8,128)(2,1)}) fusion(f32[4096,2560]{1,0:T(8,128)} %fusion.193, f32[4096,2560]{1,0:T(8,128)} %get-tuple-element.276, bf16[1,2560,896]{2,1,0:T(8,128)(2,1)} %all-gather.38.cloned.1.call-done, bf16[1,4096,896]{2,1,0:T(8,128)(2,1)} %param.12), kind=kOutput, calls=%fused_computation.173 | convolution fusion | flops 18958254080 | bytes 137756672 | tf_op jit(solution)/vmap(transpose(jvp()))/dot_general | solution.py:9
  536.2 24.9 %fusion.160 = bf16[4096,896]{0,1:T(8,128)(2,1)} fusion(bf16[1,1,4096,2560]{3,2,1,0:T(8,128)(2,1)} %get-tuple-element.551, bf16[1,896,2560]{2,1,0:T(8,128)(2,1)} %all-gather.36.cloned.1.call-done), kind=kOutput, calls=%fused_computation.182 | convolution fusion | flops 18790481920 | bytes 32899072 | tf_op jit(solution)/vmap(transpose(jvp()))/dot_general | solution.py:20
  561.2 30.8 %fusion.184 = (f32[4096]{0:T(1024)S(1)}, bf16[4096,896]{0,1:T(8,128)(2,1)}) fusion(bf16[1,1,4096,896]{2,3,1,0:T(8,128)(2,1)} %copy-done.16, bf16[4096,896]{0,1:T(8,128)(2,1)} %fusion.160, bf16[1,896,2560]{2,1,0:T(8,128)(2,1)} %all-gather.40.cloned.1.call-done, bf16[1,1,4096,2560]{3,2,1,0:T(8,128)(2,1)} %get-tuple-element.629), kind=kOutput, calls=%fused_computation.227 | convolution fusion | flops 18808827904 | bytes 47595520 | tf_op jit(solution)/vmap(transpose(jvp()))/dot_general | solution.py:21
  615.4 118.5 %while.17 = (bf16[1,1,4096,2560]{2,3,1,0:T(8,128)(2,1)}, bf16[1,1,4096,896]{3,2,1,0:T(8,128)(2,1)}, f32[1,320,896]{2,1,0:T(8,128)S(1)}, f32[1,320,896]{2,1,0:T(8...) while((bf16[1,1,4096,2560]{2,3,1,0:T(8,128)(2,1)}, ...), condition=%wide.windowed_dot_general_cond_rs.5.clone, body=%wide.windowed_dot_general_body_rs.5.clone.sunk | while | flops 9417932800 | bytes 160826096 | solution.py:9
  659.5 14.6 %collective-permute-done.22 = f32[1,320,896]{2,1,0:T(8,128)S(1)} collective-permute-done((f32[1,320,896]{2,1,0:T(8,128)S(1)}, f32[1,320,896]{2,1,0:T(8,128)S(1)}, u32[]{:S(2)}, u32[]{:S(2)}) %collective-permute-start.22) | collective-permute-done | bytes 1146912 | tf_op jit(solution)/vmap(transpose(jvp()))/dot_general | solution.py:9
  735.0 129.3 %while.14 = (bf16[1,1,4096,896]{2,3,1,0:T(8,128)(2,1)}, bf16[1,1,4096,2560]{3,2,1,0:T(8,128)(2,1)}, f32[1,112,2560]{2,1,0:T(8,128)S(1)}, f32[1,112,2560]{2,1,0:T...) while((bf16[1,1,4096,896]{2,3,1,0:T(8,128)(2,1)}, ...), condition=%wide.windowed_dot_general_cond_rs.2.clone, body=%wide.windowed_dot_general_body_rs.2.clone.sunk | while | flops 9404301312 | bytes 119931536 | solution.py:21
  752.4 23.2 %collective-permute-done.8 = f32[1,112,2560]{2,1,0:T(8,128)S(1)} collective-permute-done((f32[1,112,2560]{2,1,0:T(8,128)}, f32[1,112,2560]{2,1,0:T(8,128)S(1)}, u32[]{:S(2)}, u32[]{:S(2)}) %collective-permute-start.8) | collective-permute-done | bytes 1146912 | tf_op jit(solution)/vmap(transpose(jvp()))/dot_general | solution.py:21
  847.9 15.2 %collective-permute-done.10 = f32[1,112,2560]{2,1,0:T(8,128)S(1)} collective-permute-done((f32[1,112,2560]{2,1,0:T(8,128)S(1)}, f32[1,112,2560]{2,1,0:T(8,128)S(1)}, u32[]{:S(2)}, u32[]{:S(2)}) %collective-permute-start.10) | collective-permute-done | bytes 1146912 | tf_op jit(solution)/vmap(transpose(jvp()))/dot_general | solution.py:21
  864.3 56.3 %convert_multiply_fusion.1 = (bf16[1,1,4096,2560]{3,2,1,0:T(8,128)(2,1)}, bf16[1,1,4096,2560]{3,2,1,0:T(8,128)(2,1)}) fusion(f32[4096,2560]{1,0:T(8,128)} %fusion.212, f32[4096,2560]{1,0:T(8,128)} %get-tuple-element.269, bf16[1,2560,896]{2,1,0:T(8,128)(2,1)} %all-gather.34.cloned.1.call-done, bf16[1,1,4096,896]{2,3,1,0:T(8,128)(2,1)} %fusion.187), kind=kOutput, calls=%fused_computation.171 | convolution fusion | flops 18958254080 | bytes 137756672 | tf_op jit(solution)/vmap(transpose(jvp()))/dot_general | solution.py:9
  920.6 25.0 %fusion.156 = bf16[4096,896]{0,1:T(8,128)(2,1)} fusion(bf16[1,1,4096,2560]{3,2,1,0:T(8,128)(2,1)} %get-tuple-element.512, bf16[1,896,2560]{2,1,0:T(8,128)(2,1)} %all-gather.30.cloned.1.call-done), kind=kOutput, calls=%fused_computation.178 | convolution fusion | flops 18790481920 | bytes 32899072 | tf_op jit(solution)/vmap(transpose(jvp()))/dot_general | solution.py:20
  945.6 32.7 %fusion.181 = (bf16[1,1,4096,896]{2,3,1,0:T(8,128)(2,1)}, f32[4096]{0:T(1024)}, bf16[4096,896]{0,1:T(8,128)(2,1)}) fusion(bf16[1,4096,896]{1,2,0:T(8,128)(2,1)} %copy.1, f32[4096]{0:T(1024)S(1)} %bitcast.586, bf16[4096,896]{0,1:T(8,128)(2,1)} %fusion.156, bf16[1,896,2560]{2,1,0:T(8,128)(2,1)} %all-gather.32.cloned.1.call-done, ...), kind=kOutput, calls=%fused_computation.224 | convolution fusion | flops 18816167936 | bytes 54951936 | tf_op jit(solution)/vmap(transpose(jvp()))/dot_general | solution.py:21
  978.3 116.3 %while.15 = (bf16[1,1,4096,896]{2,3,1,0:T(8,128)(2,1)}, bf16[1,1,4096,2560]{3,2,1,0:T(8,128)(2,1)}, f32[1,112,2560]{2,1,0:T(8,128)S(1)}, f32[1,112,2560]{2,1,0:T...) while((bf16[1,1,4096,896]{2,3,1,0:T(8,128)(2,1)}, ...), condition=%wide.windowed_dot_general_cond_rs.3.clone, body=%wide.windowed_dot_general_body_rs.3.clone.sunk | while | flops 9404301312 | bytes 119931536 | solution.py:21
  1021.1 16.2 %collective-permute-done.14 = f32[1,112,2560]{2,1,0:T(8,128)S(1)} collective-permute-done((f32[1,112,2560]{2,1,0:T(8,128)S(1)}, f32[1,112,2560]{2,1,0:T(8,128)S(1)}, u32[]{:S(2)}, u32[]{:S(2)}) %collective-permute-start.14) | collective-permute-done | bytes 1146912 | tf_op jit(solution)/vmap(transpose(jvp()))/dot_general | solution.py:21
  1080.7 13.7 collective-permute-done.14
  1096.7 120.8 %while.12 = (bf16[1,1,4096,896]{2,3,1,0:T(8,128)(2,1)}, bf16[1,1,4096,2560]{3,2,1,0:T(8,128)(2,1)}, f32[1,112,2560]{2,1,0:T(8,128)S(1)}, f32[1,112,2560]{2,1,0:T...) while((bf16[1,1,4096,896]{2,3,1,0:T(8,128)(2,1)}, ...), condition=%wide.windowed_dot_general_cond_rs.clone, body=%wide.windowed_dot_general_body_rs.clone.sunk | while | flops 9404301312 | bytes 119931536 | solution.py:20
  1141.4 14.0 %collective-permute-done.2 = f32[1,112,2560]{2,1,0:T(8,128)S(1)} collective-permute-done((f32[1,112,2560]{2,1,0:T(8,128)S(1)}, f32[1,112,2560]{2,1,0:T(8,128)S(1)}, u32[]{:S(2)}, u32[]{:S(2)}) %collective-permute-start.2) | collective-permute-done | bytes 1146912 | tf_op jit(solution)/vmap(transpose(jvp()))/dot_general | solution.py:20
  1202.4 13.8 collective-permute-done.2
  1218.6 113.8 %while.13 = (bf16[1,1,4096,896]{2,3,1,0:T(8,128)(2,1)}, bf16[1,1,4096,2560]{3,2,1,0:T(8,128)(2,1)}, f32[1,112,2560]{2,1,0:T(8,128)S(1)}, f32[1,112,2560]{2,1,0:T...) while((bf16[1,1,4096,896]{2,3,1,0:T(8,128)(2,1)}, ...), condition=%wide.windowed_dot_general_cond_rs.1.clone, body=%wide.windowed_dot_general_body_rs.1.clone.sunk | while | flops 9404301312 | bytes 119931536 | solution.py:20
  1261.0 14.2 %collective-permute-done.6 = f32[1,112,2560]{2,1,0:T(8,128)S(1)} collective-permute-done((f32[1,112,2560]{2,1,0:T(8,128)S(1)}, f32[1,112,2560]{2,1,0:T(8,128)S(1)}, u32[]{:S(2)}, u32[]{:S(2)}) %collective-permute-start.6) | collective-permute-done | bytes 1146912 | tf_op jit(solution)/vmap(transpose(jvp()))/dot_general | solution.py:20
  1317.8 14.3 %collective-permute-done.6 = f32[1,112,2560]{2,1,0:T(8,128)S(1)} collective-permute-done((f32[1,112,2560]{2,1,0:T(8,128)S(1)}, f32[1,112,2560]{2,1,0:T(8,128)S(1)}, u32[]{:S(2)}, u32[]{:S(2)}) %collective-permute-start.6) | collective-permute-done | bytes 1146912 | tf_op jit(solution)/vmap(transpose(jvp()))/dot_general | solution.py:20
  (390 shorter events, 688.5 us)
Async XLA Ops:
  7.2 55.2 %all-gather.30.cloned.1.call-start = ((), (), s32[]{:S(2)}) async-start(), calls=%async_computation | async-start | bytes 5160960 | tf_op jit(solution)/vmap(jvp())/squeeze | solution.py:27
  9.7 103.1 %all-gather.32.cloned.1.call-start = ((), (), s32[]{:S(2)}) async-start(), calls=%async_computation.1 | async-start | bytes 5160960 | tf_op jit(solution)/vmap(jvp())/squeeze | solution.py:27
  12.1 151.1 %all-gather.34.cloned.1.call-start = ((), (), s32[]{:S(2)}) async-start(), calls=%async_computation.2 | async-start | bytes 5160960 | tf_op jit(solution)/vmap(jvp())/squeeze | solution.py:27
  13.3 200.2 %all-gather.36.cloned.1.call-start = ((), (), s32[]{:S(2)}) async-start(), calls=%async_computation.3 | async-start | bytes 5160960 | tf_op jit(solution)/vmap(jvp())/squeeze | solution.py:27
  13.9 249.8 %all-gather.40.cloned.1.call-start = ((), (), s32[]{:S(2)}) async-start(), calls=%async_computation.5 | async-start | bytes 5160960 | tf_op jit(solution)/vmap(jvp())/squeeze | solution.py:27
  14.5 466.5 %all-gather.38.cloned.1.call-start = ((), (), s32[]{:S(2)}) async-start(), calls=%async_computation.4 | async-start | bytes 5160960 | tf_op jit(solution)/vmap(jvp())/squeeze | solution.py:27
  363.4 28.4 %collective-permute-start.16 = (f32[1,320,896]{2,1,0:T(8,128)S(1)}, f32[1,320,896]{2,1,0:T(8,128)S(1)}, u32[]{:S(2)}, u32[]{:S(2)}) collective-permute-start(f32[1,320,896]{2,1,0:T(8,128)S(1)} %broadcast_select_fusion.32), channel_id=39, source_target_pairs={{0,1},{1,2},{2,3},{3,4},{4,5},{5,6},{6,7},{7,0},{8,9},{9,10},{10,1... | collective-permute-start | bytes 3440648 | tf_op jit(solution)/vmap(transpose(jvp()))/dot_general | solution.py:9
  392.0 28.7 %collective-permute-start.18 = (f32[1,320,896]{2,1,0:T(8,128)S(1)}, f32[1,320,896]{2,1,0:T(8,128)S(1)}, u32[]{:S(2)}, u32[]{:S(2)}) collective-permute-start(f32[1,320,896]{2,1,0:T(8,128)S(1)} %get-tuple-element.498), channel_id=41, source_target_pairs={{0,1},{1,2},{2,3},{3,4},{4,5},{5,6},{6,7},{7,0},{8,9},{9,10},{10,1... | collective-permute-start | bytes 3440648 | tf_op jit(solution)/vmap(transpose(jvp()))/dot_general | solution.py:9
  392.5 28.2 %collective-permute-start.19 = (f32[1,320,896]{2,1,0:T(8,128)S(1)}, f32[1,320,896]{2,1,0:T(8,128)S(1)}, u32[]{:S(2)}, u32[]{:S(2)}) collective-permute-start(f32[1,320,896]{2,1,0:T(8,128)S(1)} %get-tuple-element.499), channel_id=40, source_target_pairs={{0,7},{1,0},{2,1},{3,2},{4,3},{5,4},{6,5},{7,6},{8,15},{9,8},{10,9... | collective-permute-start | bytes 3440648 | tf_op jit(solution)/vmap(transpose(jvp()))/dot_general | solution.py:9
  423.4 28.1 %collective-permute-start.16 = (f32[1,320,896]{2,1,0:T(8,128)S(1)}, f32[1,320,896]{2,1,0:T(8,128)S(1)}, u32[]{:S(2)}, u32[]{:S(2)}) collective-permute-start(f32[1,320,896]{2,1,0:T(8,128)S(1)} %broadcast_select_fusion.32), channel_id=39, source_target_pairs={{0,1},{1,2},{2,3},{3,4},{4,5},{5,6},{6,7},{7,0},{8,9},{9,10},{10,1... | collective-permute-start | bytes 3440648 | tf_op jit(solution)/vmap(transpose(jvp()))/dot_general | solution.py:9
  479.5 877.2 %collective-permute-start.28 = (f32[1,320,896]{2,1,0:T(8,128)}, f32[1,320,896]{2,1,0:T(8,128)}, u32[]{:S(2)}, u32[]{:S(2)}) collective-permute-start(f32[1,320,896]{2,1,0:T(8,128)} %get-tuple-element.45), channel_id=42, source_target_pairs={{0,1},{1,2},{2,3},{3,4},{4,5},{5,6},{6,7},{7,0},{8,9},{9,10},{10,1... | collective-permute-start | bytes 3440648 | tf_op jit(solution)/vmap(transpose(jvp()))/dot_general | solution.py:9
  616.7 28.4 %collective-permute-start.20 = (f32[1,320,896]{2,1,0:T(8,128)}, f32[1,320,896]{2,1,0:T(8,128)S(1)}, u32[]{:S(2)}, u32[]{:S(2)}) collective-permute-start(f32[1,320,896]{2,1,0:T(8,128)} %broadcast_select_fusion.34), channel_id=45, source_target_pairs={{0,1},{1,2},{2,3},{3,4},{4,5},{5,6},{6,7},{7,0},{8,9},{9,10},{10,1... | collective-permute-start | bytes 3440648 | tf_op jit(solution)/vmap(transpose(jvp()))/dot_general | solution.py:9
  645.4 28.7 %collective-permute-start.22 = (f32[1,320,896]{2,1,0:T(8,128)S(1)}, f32[1,320,896]{2,1,0:T(8,128)S(1)}, u32[]{:S(2)}, u32[]{:S(2)}) collective-permute-start(f32[1,320,896]{2,1,0:T(8,128)S(1)} %get-tuple-element.507), channel_id=47, source_target_pairs={{0,1},{1,2},{2,3},{3,4},{4,5},{5,6},{6,7},{7,0},{8,9},{9,10},{10,1... | collective-permute-start | bytes 3440648 | tf_op jit(solution)/vmap(transpose(jvp()))/dot_general | solution.py:9
  645.8 28.2 %collective-permute-start.23 = (f32[1,320,896]{2,1,0:T(8,128)S(1)}, f32[1,320,896]{2,1,0:T(8,128)S(1)}, u32[]{:S(2)}, u32[]{:S(2)}) collective-permute-start(f32[1,320,896]{2,1,0:T(8,128)S(1)} %get-tuple-element.508), channel_id=46, source_target_pairs={{0,7},{1,0},{2,1},{3,2},{4,3},{5,4},{6,5},{7,6},{8,15},{9,8},{10,9... | collective-permute-start | bytes 3440648 | tf_op jit(solution)/vmap(transpose(jvp()))/dot_general | solution.py:9
  677.6 28.1 %collective-permute-start.20 = (f32[1,320,896]{2,1,0:T(8,128)}, f32[1,320,896]{2,1,0:T(8,128)S(1)}, u32[]{:S(2)}, u32[]{:S(2)}) collective-permute-start(f32[1,320,896]{2,1,0:T(8,128)} %broadcast_select_fusion.34), channel_id=45, source_target_pairs={{0,1},{1,2},{2,3},{3,4},{4,5},{5,6},{6,7},{7,0},{8,9},{9,10},{10,1... | collective-permute-start | bytes 3440648 | tf_op jit(solution)/vmap(transpose(jvp()))/dot_general | solution.py:9
  733.9 624.5 %collective-permute-start.29 = (f32[1,320,896]{2,1,0:T(8,128)}, f32[1,320,896]{2,1,0:T(8,128)}, u32[]{:S(2)}, u32[]{:S(2)}) collective-permute-start(f32[1,320,896]{2,1,0:T(8,128)} %get-tuple-element.47), channel_id=48, source_target_pairs={{0,1},{1,2},{2,3},{3,4},{4,5},{5,6},{6,7},{7,0},{8,9},{9,10},{10,1... | collective-permute-start | bytes 3440648 | tf_op jit(solution)/vmap(transpose(jvp()))/dot_general | solution.py:9
  736.1 39.4 %collective-permute-start.8 = (f32[1,112,2560]{2,1,0:T(8,128)}, f32[1,112,2560]{2,1,0:T(8,128)S(1)}, u32[]{:S(2)}, u32[]{:S(2)}) collective-permute-start(f32[1,112,2560]{2,1,0:T(8,128)} %broadcast_select_fusion.28), channel_id=27, source_target_pairs={{0,1},{1,2},{2,3},{3,4},{4,5},{5,6},{6,7},{7,0},{8,9},{9,10},{10,1... | collective-permute-start | bytes 3440648 | tf_op jit(solution)/vmap(transpose(jvp()))/dot_general | solution.py:21
  737.2 38.4 %collective-permute-start.9 = (f32[1,112,2560]{2,1,0:T(8,128)S(1)}, f32[1,112,2560]{2,1,0:T(8,128)S(1)}, u32[]{:S(2)}, u32[]{:S(2)}) collective-permute-start(f32[1,112,2560]{2,1,0:T(8,128)S(1)} %broadcast_select_fusion.29), channel_id=26, source_target_pairs={{0,7},{1,0},{2,1},{3,2},{4,3},{5,4},{6,5},{7,6},{8,15},{9,8},{10,9... | collective-permute-start | bytes 3440648 | tf_op jit(solution)/vmap(transpose(jvp()))/dot_general | solution.py:21
  805.4 29.0 %collective-permute-start.8 = (f32[1,112,2560]{2,1,0:T(8,128)}, f32[1,112,2560]{2,1,0:T(8,128)S(1)}, u32[]{:S(2)}, u32[]{:S(2)}) collective-permute-start(f32[1,112,2560]{2,1,0:T(8,128)} %broadcast_select_fusion.28), channel_id=27, source_target_pairs={{0,1},{1,2},{2,3},{3,4},{4,5},{5,6},{6,7},{7,0},{8,9},{9,10},{10,1... | collective-permute-start | bytes 3440648 | tf_op jit(solution)/vmap(transpose(jvp()))/dot_general | solution.py:21
  834.8 28.3 %collective-permute-start.10 = (f32[1,112,2560]{2,1,0:T(8,128)S(1)}, f32[1,112,2560]{2,1,0:T(8,128)S(1)}, u32[]{:S(2)}, u32[]{:S(2)}) collective-permute-start(f32[1,112,2560]{2,1,0:T(8,128)S(1)} %get-tuple-element.480), channel_id=29, source_target_pairs={{0,1},{1,2},{2,3},{3,4},{4,5},{5,6},{6,7},{7,0},{8,9},{9,10},{10,1... | collective-permute-start | bytes 3440648 | tf_op jit(solution)/vmap(transpose(jvp()))/dot_general | solution.py:21
  835.1 28.0 %collective-permute-start.11 = (f32[1,112,2560]{2,1,0:T(8,128)S(1)}, f32[1,112,2560]{2,1,0:T(8,128)S(1)}, u32[]{:S(2)}, u32[]{:S(2)}) collective-permute-start(f32[1,112,2560]{2,1,0:T(8,128)S(1)} %get-tuple-element.481), channel_id=28, source_target_pairs={{0,7},{1,0},{2,1},{3,2},{4,3},{5,4},{6,5},{7,6},{8,15},{9,8},{10,9... | collective-permute-start | bytes 3440648 | tf_op jit(solution)/vmap(transpose(jvp()))/dot_general | solution.py:21
  864.3 495.4 %collective-permute-start.26 = (f32[1,112,2560]{2,1,0:T(8,128)}, f32[1,112,2560]{2,1,0:T(8,128)}, u32[]{:S(2)}, u32[]{:S(2)}) collective-permute-start(f32[1,112,2560]{2,1,0:T(8,128)} %get-tuple-element.41), channel_id=30, source_target_pairs={{0,1},{1,2},{2,3},{3,4},{4,5},{5,6},{6,7},{7,0},{8,9},{9,10},{10,1... | collective-permute-start | bytes 3440648 | tf_op jit(solution)/vmap(transpose(jvp()))/dot_general | solution.py:21
  979.8 27.7 %collective-permute-start.12 = (f32[1,112,2560]{2,1,0:T(8,128)}, f32[1,112,2560]{2,1,0:T(8,128)S(1)}, u32[]{:S(2)}, u32[]{:S(2)}) collective-permute-start(f32[1,112,2560]{2,1,0:T(8,128)} %broadcast_select_fusion.30), channel_id=33, source_target_pairs={{0,1},{1,2},{2,3},{3,4},{4,5},{5,6},{6,7},{7,0},{8,9},{9,10},{10,1... | collective-permute-start | bytes 3440648 | tf_op jit(solution)/vmap(transpose(jvp()))/dot_general | solution.py:21
  1007.9 29.3 %collective-permute-start.14 = (f32[1,112,2560]{2,1,0:T(8,128)S(1)}, f32[1,112,2560]{2,1,0:T(8,128)S(1)}, u32[]{:S(2)}, u32[]{:S(2)}) collective-permute-start(f32[1,112,2560]{2,1,0:T(8,128)S(1)} %get-tuple-element.489), channel_id=35, source_target_pairs={{0,1},{1,2},{2,3},{3,4},{4,5},{5,6},{6,7},{7,0},{8,9},{9,10},{10,1... | collective-permute-start | bytes 3440648 | tf_op jit(solution)/vmap(transpose(jvp()))/dot_general | solution.py:21
  1008.3 29.0 %collective-permute-start.15 = (f32[1,112,2560]{2,1,0:T(8,128)S(1)}, f32[1,112,2560]{2,1,0:T(8,128)S(1)}, u32[]{:S(2)}, u32[]{:S(2)}) collective-permute-start(f32[1,112,2560]{2,1,0:T(8,128)S(1)} %get-tuple-element.490), channel_id=34, source_target_pairs={{0,7},{1,0},{2,1},{3,2},{4,3},{5,4},{6,5},{7,6},{8,15},{9,8},{10,9... | collective-permute-start | bytes 3440648 | tf_op jit(solution)/vmap(transpose(jvp()))/dot_general | solution.py:21
  1038.6 28.5 %collective-permute-start.12 = (f32[1,112,2560]{2,1,0:T(8,128)}, f32[1,112,2560]{2,1,0:T(8,128)S(1)}, u32[]{:S(2)}, u32[]{:S(2)}) collective-permute-start(f32[1,112,2560]{2,1,0:T(8,128)} %broadcast_select_fusion.30), channel_id=33, source_target_pairs={{0,1},{1,2},{2,3},{3,4},{4,5},{5,6},{6,7},{7,0},{8,9},{9,10},{10,1... | collective-permute-start | bytes 3440648 | tf_op jit(solution)/vmap(transpose(jvp()))/dot_general | solution.py:21
  1097.8 28.9 %collective-permute-start = (f32[1,112,2560]{2,1,0:T(8,128)}, f32[1,112,2560]{2,1,0:T(8,128)}, u32[]{:S(2)}, u32[]{:S(2)}) collective-permute-start(f32[1,112,2560]{2,1,0:T(8,128)} %broadcast_select_fusion.24), channel_id=15, source_target_pairs={{0,1},{1,2},{2,3},{3,4},{4,5},{5,6},{6,7},{7,0},{8,9},{9,10},{10,1... | collective-permute-start | bytes 3440648 | tf_op jit(solution)/vmap(transpose(jvp()))/dot_general | solution.py:20
  1098.9 27.8 %collective-permute-start.1 = (f32[1,112,2560]{2,1,0:T(8,128)}, f32[1,112,2560]{2,1,0:T(8,128)S(1)}, u32[]{:S(2)}, u32[]{:S(2)}) collective-permute-start(f32[1,112,2560]{2,1,0:T(8,128)} %broadcast_select_fusion.25), channel_id=14, source_target_pairs={{0,7},{1,0},{2,1},{3,2},{4,3},{5,4},{6,5},{7,6},{8,15},{9,8},{10,9... | collective-permute-start | bytes 3440648 | tf_op jit(solution)/vmap(transpose(jvp()))/dot_general | solution.py:20
  1159.0 28.6 %collective-permute-start = (f32[1,112,2560]{2,1,0:T(8,128)}, f32[1,112,2560]{2,1,0:T(8,128)}, u32[]{:S(2)}, u32[]{:S(2)}) collective-permute-start(f32[1,112,2560]{2,1,0:T(8,128)} %broadcast_select_fusion.24), channel_id=15, source_target_pairs={{0,1},{1,2},{2,3},{3,4},{4,5},{5,6},{6,7},{7,0},{8,9},{9,10},{10,1... | collective-permute-start | bytes 3440648 | tf_op jit(solution)/vmap(transpose(jvp()))/dot_general | solution.py:20
  1276.6 27.7 %collective-permute-start.4 = (f32[1,112,2560]{2,1,0:T(8,128)}, f32[1,112,2560]{2,1,0:T(8,128)S(1)}, u32[]{:S(2)}, u32[]{:S(2)}) collective-permute-start(f32[1,112,2560]{2,1,0:T(8,128)} %broadcast_select_fusion.26), channel_id=21, source_target_pairs={{0,1},{1,2},{2,3},{3,4},{4,5},{5,6},{6,7},{7,0},{8,9},{9,10},{10,1... | collective-permute-start | bytes 3440648 | tf_op jit(solution)/vmap(transpose(jvp()))/dot_general | solution.py:20
  1332.4 28.8 %collective-permute-start.27 = (f32[1,112,2560]{2,1,0:T(8,128)}, f32[1,112,2560]{2,1,0:T(8,128)}, u32[]{:S(2)}, u32[]{:S(2)}) collective-permute-start(f32[1,112,2560]{2,1,0:T(8,128)} %copy-done.20), channel_id=36, source_target_pairs={{0,1},{1,2},{2,3},{3,4},{4,5},{5,6},{6,7},{7,0},{8,9},{9,10},{10,1... | collective-permute-start | bytes 3440648 | tf_op jit(solution)/vmap(transpose(jvp()))/dot_general | solution.py:21
  1356.8 29.4 %collective-permute-start.25 = (f32[1,112,2560]{2,1,0:T(8,128)}, f32[1,112,2560]{2,1,0:T(8,128)S(1)}, u32[]{:S(2)}, u32[]{:S(2)}) collective-permute-start(f32[1,112,2560]{2,1,0:T(8,128)} %copy-done.18), channel_id=24, source_target_pairs={{0,1},{1,2},{2,3},{3,4},{4,5},{5,6},{6,7},{7,0},{8,9},{9,10},{10,1... | collective-permute-start | bytes 3440648 | tf_op jit(solution)/vmap(transpose(jvp()))/dot_general | solution.py:20
  (99 other events, 3018.3 us)
Sparse Core Ops, SparseCore 0:
  9.8 52.5 all-gather.29
  64.0 48.7 all-gather.31
  114.4 48.7 all-gather.33
  164.7 48.7 all-gather.35
  215.0 48.7 all-gather.39
  265.2 48.7 all-gather.37
where the time goes:
time: 1410 us; the launch traced here: 1390 us
  matrix products  651 us (46%)
  waiting for transfers between devices  402 us (29%)
  local copies, waits for them, and re-layouts  128 us (9%)
  starting transfers between devices  88.9 us (6%)
  other arithmetic  86.3 us (6%)
  loops' own time  23.8 us (2%)
  between operations  14.7 us (1%)
    dot_general x12, matrix products, layer(): up = jnp.dot(a, w['w_up'], preferred_element_type=jnp.float32)  235 us
    dot_general x11, matrix products, matmul(): jnp.dot(a, w, preferred_element_type=jnp.float32).astype(jnp.bfloat16)  228 us
    dot_general x12, matrix products, layer(): gate = jnp.dot(a, w['w_gate'], preferred_element_type=jnp.float32)  188 us
    dot_general x18, waiting for transfers between devices, layer(): gate = jnp.dot(a, w['w_gate'], preferred_element_type=jnp.float32)  123 us
    dot_general x18, waiting for transfers between devices, layer(): up = jnp.dot(a, w['w_up'], preferred_element_type=jnp.float32)  115 us
    unnamed x77, local copies, waits for them, and re-layouts  114 us
    dot_general x18, waiting for transfers between devices, matmul(): jnp.dot(a, w, preferred_element_type=jnp.float32).astype(jnp.bfloat16)  89.6 us
    squeeze x6, waiting for transfers between devices, stack(): h = layer(h, {name: w[number] for name, w in weights.items()})  72.3 us
  transfers between devices with their start and end apart: 60, of which 31 were waited for; matrix products, arithmetic and copies ran while one was open for 61% of the time, Pallas kernels for 0%

commit v1 on v0

v1 whole, which is shorter than its diff:
```python
import functools

import jax
import jax.numpy as jnp
from jax import lax
from jax.experimental import pallas as pl
from jax.experimental.pallas import tpu as pltpu
from jax.sharding import PartitionSpec as P

MESH = pl.DeviceIdType.MESH
F32, BF16 = jnp.float32, jnp.bfloat16
NC = 10
VMEM = 67_000_000
TILE = 512
WIDE = 1024


def dot(a, b):
    return jnp.dot(a, b, preferred_element_type=F32)


def dot_nt(a, b):
    return lax.dot_general(a, b, (((1,), (1,)), ((), ())), preferred_element_type=F32)


def sigmoid(x):
    return 0.5 * jnp.tanh(0.5 * x) + 0.5


def forward_kernel(a, wg, wu, wd, out, acc, wgt, wut, wdt):
    step = pl.program_id(0)
    c = wgt.shape[0]
    tokens = a.shape[1]
    wgt[...] = wg[0].T
    wut[...] = wu[0].T
    wdt[...] = wd[0].reshape(c, a.shape[0]).T

    @pl.when(step == 0)
    def _():
        acc[...] = jnp.zeros_like(acc)

    def body(t, _):
        for k in range(2):
            at = pl.ds(pl.multiple_of((2 * t + k) * TILE, TILE), TILE)
            x = a[:, at]
            gate, up = dot(wgt[...], x), dot(wut[...], x)
            hid = (gate * sigmoid(gate) * up).astype(BF16)
            acc[:, at] += dot(wdt[...], hid)
        return 0

    lax.fori_loop(0, tokens // TILE // 2, body, 0)

    @pl.when(step == NC - 1)
    def _():
        out[...] = acc[...].astype(BF16)


def weight_specs(d, c):
    at = lambda s: jnp.minimum(s, NC - 1)
    cols = pl.BlockSpec((1, d, c), lambda s: (at(s) // 2, 0, at(s) % 2))
    rows = pl.BlockSpec((1, 8, c // 8, d), lambda s: (at(s) // 2, 0, at(s) % 2, 0))
    return [cols, cols, rows]


def forward(a, wg, wu, wd):
    d, tokens = a.shape
    c = wg.shape[2] // 2
    whole = pl.BlockSpec((d, tokens), lambda s: (0, 0), pipeline_mode=pl.Buffered(1))
    flops = 6 * d * tokens * c * NC
    return pl.pallas_call(
        forward_kernel,
        grid=(NC,),
        out_shape=jax.ShapeDtypeStruct((d, tokens), BF16),
        in_specs=[whole, *weight_specs(d, c)],
        out_specs=whole,
        scratch_shapes=[
            pltpu.VMEM((d, tokens), F32),
            pltpu.VMEM((c, d), BF16),
            pltpu.VMEM((c, d), BF16),
            pltpu.VMEM((d, c), BF16),
        ],
        compiler_params=pltpu.CompilerParams(vmem_limit_bytes=VMEM),
        cost_estimate=pl.CostEstimate(flops=flops, bytes_accessed=4 * d * tokens, transcendentals=0),
        name="layer_forward",
    )(a, wg, wu, wd)


def backward_kernel(a, dh, wg, wu, wd, da, gu_out, d_out,
                    acc, wt, wgu, hid, dgu, gu, dd,
                    sa_gu, sa_d, ra_gu, ra_d, ka_gu, ka_d,
                    sb_gu, sb_d, rb_gu, rb_d, kb_gu, kb_d,
                    sc_gu, sc_d, rc_gu, rc_d, o_gu, o_d,
                    send, recv, out_sem):
    step = pl.program_id(0)
    me = lax.axis_index("dp")
    core, z0, z1 = me % 2, (me // 2) % 2, me // 4
    partners = (me + 1 - 2 * core, me + 2 - 4 * z0, me + 4 - 8 * z1)
    d, tokens = a.shape
    c = hid.shape[0]

    @pl.when(step == 0)
    def _():
        barrier = pltpu.get_barrier_semaphore()
        for p in partners:
            pl.semaphore_signal(barrier, 1, device_id={"dp": p}, device_id_type=MESH)
        pl.semaphore_wait(barrier, 3)
        acc[...] = jnp.zeros_like(acc)

    def copies(stage, slot):
        pairs = (((sa_gu, ra_gu), (sa_d, ra_d)), ((sb_gu, rb_gu), (sb_d, rb_d)), ((sc_gu, rc_gu), (sc_d, rc_d)))[stage]
        return [
            pltpu.make_async_remote_copy(
                src_ref=s, dst_ref=r.at[slot], send_sem=send.at[stage, n], recv_sem=recv.at[stage, n, slot],
                device_id={"dp": partners[stage]}, device_id_type=MESH)
            for n, (s, r) in enumerate(pairs)
        ]

    def outs(chunk):
        return [pltpu.make_async_copy(o_gu, gu_out.at[chunk], out_sem.at[0]),
                pltpu.make_async_copy(o_d, d_out.at[chunk], out_sem.at[1])]

    @pl.when(step < NC)
    def _():
        wt[:c] = wg[0].T
        wt[c:] = wu[0].T
        wgu[:, :c] = wg[0]
        wgu[:, c:] = wu[0]

        def body(t, _):
            for k in range(2):
                at = pl.ds(pl.multiple_of((2 * t + k) * TILE, TILE), TILE)
                x = a[:, at]
                gate, up = dot(wt[:c], x), dot(wt[c:], x)
                by_hid = dot(wd[0].reshape(c, d), dh[:, at]).astype(BF16).astype(F32)
                sig = sigmoid(gate)
                silu = gate * sig
                hid[:, at] = (silu * up).astype(BF16)
                dgu[:c, at] = (by_hid * up * (sig + silu * (1.0 - sig))).astype(BF16)
                dgu[c:, at] = (by_hid * silu).astype(BF16)
            return 0

        lax.fori_loop(0, tokens // TILE // 2, body, 0)

    @pl.when(step >= 4)
    def _():
        for copy in outs(step - 4):
            copy.wait()

    @pl.when(step >= 3)
    def _():
        slot = (step - 3) % 2
        for copy in copies(2, slot):
            copy.wait()
        o_gu[...] = (kb_gu[z1] + rc_gu[slot].astype(F32)).astype(BF16)
        o_d[...] = (kb_d[z1] + rc_d[slot].astype(F32)).astype(BF16)
        for copy in outs(step - 3):
            copy.start()

    @pl.when((step >= 2) & (step < NC + 2))
    def _():
        slot = (step - 2) % 2
        for copy in copies(1, slot):
            copy.wait()
        for half in range(2):
            kb_gu[half] = ka_gu[half, z0] + rb_gu[slot, half].astype(F32)
            kb_d[half] = ka_d[half, z0] + rb_d[slot, half].astype(F32)
        sc_gu[...] = kb_gu[1 - z1].astype(BF16)
        sc_d[...] = kb_d[1 - z1].astype(BF16)
        for copy in copies(2, slot):
            copy.start()

    @pl.when((step >= 1) & (step < NC + 1))
    def _():
        slot = (step - 1) % 2
        for copy in copies(0, slot):
            copy.wait()
        for i in range(2):
            for j in range(2):
                ka_gu[i, j] = gu[i, j, core] + ra_gu[slot, i, j].astype(F32)
                ka_d[i, j] = dd[i, j, core] + ra_d[slot, i, j].astype(F32)
            sb_gu[i] = ka_gu[i, 1 - z0].astype(BF16)
            sb_d[i] = ka_d[i, 1 - z0].astype(BF16)
        for copy in copies(1, slot):
            copy.start()

    @pl.when(step < NC)
    def _():
        def body(t, _):
            at = pl.ds(pl.multiple_of(t * WIDE, WIDE), WIDE)
            g = dgu[:, at]
            acc[:, at] += dot(wgu[...], g)
            return 0

        lax.fori_loop(0, tokens // WIDE, body, 0)

        shape = gu.shape
        gu[...] = dot_nt(a[...], dgu[...]).reshape(shape)
        dd[...] = dot_nt(dh[...], hid[...]).T.reshape(dd.shape)
        for i in range(2):
            for j in range(2):
                sa_gu[i, j] = gu[i, j, 1 - core].astype(BF16)
                sa_d[i, j] = dd[i, j, 1 - core].astype(BF16)
        for copy in copies(0, step % 2):
            copy.start()

    @pl.when(step == NC - 1)
    def _():
        da[...] = acc[...].astype(BF16)

    @pl.when(step == NC + 2)
    def _():
        for copy in outs(NC - 1):
            copy.wait()


def backward(a, dh, wg, wu, wd, number):
    d, tokens = a.shape
    c = wg.shape[2] // 2
    m, n = d // 8, c // 8
    whole = pl.BlockSpec((d, tokens), lambda s: (0, 0), pipeline_mode=pl.Buffered(1))
    anywhere = pl.BlockSpec(memory_space=pl.ANY)
    both = lambda *lead, dtype: [pltpu.VMEM((*lead, m, 2 * c), dtype), pltpu.VMEM((*lead, n, d), dtype)]
    return pl.pallas_call(
        backward_kernel,
        grid=(NC + 3,),
        out_shape=[
            jax.ShapeDtypeStruct((d, tokens), BF16),
            jax.ShapeDtypeStruct((NC, m, 2 * c), BF16),
            jax.ShapeDtypeStruct((NC, n, d), BF16),
        ],
        in_specs=[whole, whole, *weight_specs(d, c)],
        out_specs=[whole, anywhere, anywhere],
        scratch_shapes=[
            pltpu.VMEM((d, tokens), F32),
            pltpu.VMEM((2 * c, d), BF16),
            pltpu.VMEM((d, 2 * c), BF16),
            pltpu.VMEM((c, tokens), BF16),
            pltpu.VMEM((2 * c, tokens), BF16),
            *both(2, 2, 2, dtype=F32),
            *both(2, 2, dtype=BF16), *both(2, 2, 2, dtype=BF16), *both(2, 2, dtype=F32),
            *both(2, dtype=BF16), *both(2, 2, dtype=BF16), *both(2, dtype=F32),
            *both(dtype=BF16), *both(2, dtype=BF16), *both(dtype=BF16),
            pltpu.SemaphoreType.DMA((3, 2)),
            pltpu.SemaphoreType.DMA((3, 2, 2)),
            pltpu.SemaphoreType.DMA((2,)),
        ],
        compiler_params=pltpu.CompilerParams(vmem_limit_bytes=VMEM, collective_id=1 + number, has_side_effects=True),
        cost_estimate=pl.CostEstimate(flops=16 * d * tokens * c * NC, bytes_accessed=6 * d * tokens, transcendentals=0),
        name=f"layer_backward_{number}",
    )(a, dh, wg, wu, wd)


def gather_kernel(cols, rows, cols_all, rows_all, send, recv, local):
    me, rep = lax.axis_index("dp"), lax.axis_index("rep")
    core, z0, z1 = me % 2, (me // 2) % 2, me // 4
    x, y = rep // 2, rep % 2
    sibling, near, far = me + 1 - 2 * core, me + 2 - 4 * z0, me + 4 - 8 * z1
    both = far + 2 - 4 * z0
    by_x, by_y = rep + 2 - 4 * x, rep + 1 - 2 * y
    q, r = cols.shape[-1] // 4, rows.shape[-2] // 4

    barrier = pltpu.get_barrier_semaphore()
    peers = [{"dp": far}, {"dp": near}, {"rep": by_x}, {"rep": by_y}, {"dp": sibling}]
    for p in peers:
        pl.semaphore_signal(barrier, 1, device_id=p, device_id_type=MESH)
    pl.semaphore_wait(barrier, len(peers))

    mine = []
    for i in range(4):
        mine.append(pltpu.make_async_copy(cols.at[i], cols_all.at[i, :, me], local.at[i]))
    for i in range(2):
        mine.append(pltpu.make_async_copy(rows.at[i], rows_all.at[i, :, me], local.at[4 + i]))
    for copy in mine:
        copy.start()

    pieces = []
    for layer in range(2):
        pieces += [("c", 2 * layer), ("c", 2 * layer + 1), ("r", layer)]

    def part(piece, owner, quarter):
        kind, i = pieces[piece]
        if kind == "c":
            return cols_all.at[i, :, owner, :, pl.ds(pl.multiple_of(quarter * q, q), q)]
        return rows_all.at[i, :, owner, pl.ds(pl.multiple_of(quarter * r, r), r), :]

    def first(piece):
        kind, i = pieces[piece]
        if kind == "c":
            return cols.at[i, :, :, pl.ds(pl.multiple_of(rep * q, q), q)]
        return rows.at[i, :, pl.ds(pl.multiple_of(rep * r, r), r), :]

    def shard(piece, owner):
        kind, i = pieces[piece]
        return cols_all.at[i, :, owner] if kind == "c" else rows_all.at[i, :, owner]

    def stage(piece, s):
        flip = piece in (1, 3, 5)
        one, two = (by_y, by_x) if flip else (by_x, by_y)
        if s == 0:
            return [(first(piece), part(piece, me, rep), {"dp": far}, 0)]
        if s == 1:
            return [(first(piece), part(piece, me, rep), {"dp": near}, 1),
                    (part(piece, far, rep), part(piece, far, rep), {"dp": near}, 2)]
        if s == 2:
            return [(part(piece, o, rep), part(piece, o, rep), {"rep": one}, 3 + n) for n, o in enumerate((far, near, both))]
        if s == 3:
            return [(part(piece, o, w), part(piece, o, w), {"rep": two}, 6 + 2 * n + k)
                    for n, o in enumerate((far, near, both)) for k, w in enumerate((rep, one))]
        own = [(shard(piece, o), shard(piece, o), {"dp": sibling}, 13 + n) for n, o in enumerate((far, near, both))]
        kind, i = pieces[piece]
        src = cols.at[i] if kind == "c" else rows.at[i]
        return [(src, shard(piece, me), {"dp": sibling}, 12)] + own

    def copies(piece, s):
        return [pltpu.make_async_remote_copy(src_ref=a, dst_ref=b, send_sem=send.at[piece, n], recv_sem=recv.at[piece, n],
                                             device_id=dev, device_id_type=MESH) for a, b, dev, n in stage(piece, s)]

    count = len(pieces)
    for wave in range(count + 5):
        for s in reversed(range(5)):
            piece = wave - s
            if 0 <= piece < count:
                if s:
                    for copy in copies(piece, s - 1):
                        copy.wait_recv()
                for copy in copies(piece, s):
                    copy.start()
        piece = wave - 5
        if 0 <= piece < count:
            for copy in copies(piece, 4):
                copy.wait_recv()
    for piece in range(count):
        for s in range(5):
            for copy in copies(piece, s):
                copy.wait_send()
    for copy in mine:
        copy.wait()


def gather(cols, rows):
    inside = pl.BlockSpec(memory_space=pltpu.VMEM)
    anywhere = pl.BlockSpec(memory_space=pl.ANY)
    return pl.pallas_call(
        gather_kernel,
        out_shape=[
            jax.ShapeDtypeStruct((*cols.shape[:2], 8, *cols.shape[2:]), BF16),
            jax.ShapeDtypeStruct((*rows.shape[:2], 8, *rows.shape[2:]), BF16),
        ],
        in_specs=[inside, inside],
        out_specs=[anywhere, anywhere],
        scratch_shapes=[pltpu.SemaphoreType.DMA((6, 16)), pltpu.SemaphoreType.DMA((6, 16)), pltpu.SemaphoreType.DMA((6,))],
        compiler_params=pltpu.CompilerParams(collective_id=0, has_side_effects=True, vmem_limit_bytes=VMEM),
        cost_estimate=pl.CostEstimate(flops=10**11, bytes_accessed=6 * 10**7, transcendentals=0),
        name="gather_weights",
    )(cols, rows)


def scale_of(h):
    wide = h.astype(F32)
    return lax.rsqrt(jnp.mean(wide**2, 0, keepdims=True) + 1e-6)


def normed(h):
    return (h.astype(F32) * scale_of(h)).astype(BF16)


def through_norm(h, by_a, by_h):
    wide, g, scale = h.astype(F32), by_a.astype(F32), scale_of(h)
    back = g * scale - wide * (scale**3 * jnp.mean(g * wide, 0, keepdims=True))
    return (by_h.astype(F32) + back.astype(BF16).astype(F32)).astype(BF16)


def solution(mesh):
    def local(x, dy, wg, wu, wd):
        layers, m, ff = wg.shape
        d = wd.shape[2]
        n = wd.shape[1] // NC
        h0, by_y = x[0].T, dy[0].T

        def ordered(w):
            w = w.reshape(layers, m, 8, NC // 2, 2, n).transpose(0, 3, 1, 4, 2, 5)
            return w.reshape(layers, NC // 2, m, 16 * n)

        cols = jnp.stack([ordered(wg), ordered(wu)], 1).reshape(2 * layers, NC // 2, m, 16 * n)
        rows = wd.reshape(layers, NC // 2, 2 * n, d)
        cols, rows = gather(cols, rows)
        cols = cols.reshape(layers, 2, NC // 2, d, 16 * n)
        weights = [(cols[i, 0], cols[i, 1], rows[i]) for i in range(layers)]

        a0 = normed(h0)
        h1 = (h0.astype(F32) + forward(a0, *weights[0]).astype(F32)).astype(BF16)
        a1 = normed(h1)
        by_a1, gu1, d1 = backward(a1, by_y, *weights[1], 1)
        by_h1 = through_norm(h1, by_a1, by_y)
        by_a0, gu0, d0 = backward(a0, by_h1, *weights[0], 0)
        by_x = through_norm(h0, by_a0, by_h1).T[None]

        def restored(*both):
            w = jnp.stack(both).reshape(layers, NC, m, 8, n).transpose(0, 2, 3, 1, 4)
            return w.reshape(layers, m, ff)

        half = 8 * n
        return (by_x, restored(gu0[..., :half], gu1[..., :half]), restored(gu0[..., half:], gu1[..., half:]),
                jnp.stack([d0, d1]).reshape(layers, NC * n, d))

    seq = P(("rep", "dp"), None, None)
    w = P(None, "dp", None)
    g = P("rep", "dp", None)
    return jax.shard_map(local, mesh=mesh, in_specs=(seq, seq, w, w, w), out_specs=(seq, g, g, g), check_vma=False)
```

time: 1410 us -> 904 us (0.64)
  Pallas kernels: 0 us -> 750 us
  matrix products: 651 us -> 0 us
  waiting for transfers between devices: 402 us -> 0 us
  starting transfers between devices: 88.9 us -> 0 us
  local copies, waits for them, and re-layouts: 128 us -> 71.3 us
  loops' own time: 23.8 us -> 0 us
    pallas_call x0 -> x4, Pallas kernels: none -> 750 us  [the longest x2 456 us: backward(): pl.pallas_call(backward_kernel, grid=(NC + 3,), out_shape=[jax.ShapeDtype...]
    dot_general x35 -> x0, matrix products: 651 us -> none  [the longest x12 235 us: layer(): up = jnp.dot(a, w['w_up'], preferred_element_type=jnp.float32)]
    dot_general x54 -> x0, waiting for transfers between devices: 328 us -> none  [the longest x18 123 us: layer(): gate = jnp.dot(a, w['w_gate'], preferred_element_type=jnp.float32)]
    dot_general x54 -> x0, starting transfers between devices: 88.6 us -> none  [the longest x18 31.2 us: matmul(): jnp.dot(a, w, preferred_element_type=jnp.float32).astype(jnp.bfloat16)]
    squeeze x6 -> x0, waiting for transfers between devices: 72.3 us -> none  [stack(): h = layer(h, {name: w[number] for name, w in weights.items()})]
    unnamed x77 -> x39, local copies, waits for them, and re-layouts: 114 us -> 42.1 us
    dot_general x60 -> x0, other arithmetic: 42.7 us -> none
    reduce_sum x1 -> x4, other arithmetic: 4.59 us -> 33.7 us  [the longest x2 17 us: scale_of(): return lax.rsqrt(jnp.mean(wide ** 2, 0, keepdims=True) + 1e-06)]
  transfers between devices with their start and end apart: 60 -> 0, of which waited for: 31 -> 0; matrix products, arithmetic and copies ran while one was open for 61% -> 0% of each run, Pallas kernels for 0% -> 0%
where the time goes in v1:
time: 904 us; the launch traced here: 896 us
  Pallas kernels  750 us (83%)
  other arithmetic  73.9 us (8%)
  local copies, waits for them, and re-layouts  71.3 us (8%)
    pallas_call x2, Pallas kernels, backward(): pl.pallas_call(backward_kernel, grid=(NC + 3,), out_shape=[jax.ShapeDtype...  456 us
    pallas_call x1, Pallas kernels, gather(): pl.pallas_call(gather_kernel, out_shape=[jax.ShapeDtypeStruct((*cols.shap...  200 us
    pallas_call x1, Pallas kernels, forward(): pl.pallas_call(forward_kernel, grid=(NC,), out_shape=jax.ShapeDtypeStruct...  93.3 us
    unnamed x39, local copies, waits for them, and re-layouts  42.1 us
    squeeze x2, local copies, waits for them, and re-layouts, local(): weights = [(cols[i, 0], cols[i, 1], rows[i]) for i in range(layers)]  19.2 us

profile of v1, /device:TPU:0, one launch (start us, length us, event | category | flops | bytes accessed | tf_op | source)
XLA Modules:
  0.0 896.4 jit_solution(17352324150290467009)
XLA Ops:
  0.6 1.7 copy.18
  2.4 1.4 copy.19
  3.7 1.7 copy.20
  5.8 1.9 pad_maximum_fusion
  7.7 2.5 copy.22
  10.2 10.8 %copy.17 = bf16[1,4096,896]{1,2,0:T(8,128)(2,1)} copy(bf16[1,4096,896]{2,1,0:T(8,128)(2,1)} %param.5) | data formatting | bytes 14680064 | tf_op args[0]
  21.0 4.7 fusion.12
  25.7 0.6 copy-done.4
  26.4 0.6 copy-done.8
  27.0 5.3 fusion.13.a
  32.2 10.7 %copy.16 = bf16[1,4096,896]{1,2,0:T(8,128)(2,1)} copy(bf16[1,4096,896]{2,1,0:T(8,128)(2,1)} %param.6) | data formatting | bytes 14680064 | tf_op args[1]
  43.0 200.4 %gather_weights.1 = (bf16[4,5,8,112,512]{4,3,2,1,0:T(8,128)(2,1)}, bf16[2,5,8,64,896]{4,3,2,1,0:T(8,128)(2,1)}) custom-call(bf16[4,5,112,512]{3,2,1,0:T(8,128)(2,1)} %bitcast.90, bf16[2,5,64,896]{3,2,1,0:T(8,128)(2,1)} %bitcast.93), custom_call_target="tpu_custom_call" | custom-call | flops 99999997952 | bytes 60000000 | tf_op jit(solution)/shard_map/gather_weights/pallas_call | solution.py:343
  243.3 14.4 %slice_bitcast_fusion = (bf16[5,896,512]{2,1,0:T(8,128)(2,1)}, bf16[5,896,512]{2,1,0:T(8,128)(2,1)}, bf16[5,896,512]{2,1,0:T(8,128)(2,1)}, bf16[5,896,512]{2,1,0:T(8,128)(2,1)}) fusion(bf16[2,2,5,896,512]{4,3,2,1,0:T(8,128)(2,1)} %bitcast.79), kind=kLoop, calls=%fused_computation.26 | loop fusion | bytes 36700160 | tf_op jit(solution)/shard_map/squeeze | solution.py:388
  257.8 1.0 copy-done.1
  258.7 4.8 slice_bitcast_fusion.4
  263.5 93.3 %layer_forward.1 = bf16[896,4096]{1,0:T(8,128)(2,1)} custom-call(bf16[896,4096]{1,0:T(8,128)(2,1)} %fusion.13.a, bf16[5,896,512]{2,1,0:T(8,128)(2,1)} %get-tuple-element.33.wg, bf16[5,896,512]{2,1,0:T(8,128)(2,1)} %get-tuple-element.32.wu, bf16[5,8,64,896]{3,2,1,0:T(8,128)(2,1)} %get-tuple-element.35.wd), custom_call_target="tpu_custom_call" | custom-call | flops 56371445760 | bytes 14680064 | tf_op jit(solution)/shard_map/layer_forward/pallas_call | solution.py:70
  356.8 12.3 %fusion.5 = (f32[4096]{0:T(1024)S(1)}, bf16[896,4096]{1,0:T(8,128)(2,1)}) fusion(bf16[896,4096]{1,0:T(8,128)(2,1)} %layer_forward.1, bf16[1,4096,896]{1,2,0:T(8,128)(2,1)} %copy.17), kind=kLoop, calls=%fused_computation.12 | loop fusion | flops 25686016 | bytes 22036480 | tf_op jit(solution)/shard_map/reduce_sum | solution.py:360
  369.1 0.6 copy-done.6
  369.8 0.6 copy-done.10
  370.4 8.4 fusion.6.a
  378.7 228.7 %layer_backward_1.1 = (bf16[896,4096]{1,0:T(8,128)(2,1)}, bf16[10,112,512]{2,1,0:T(8,128)(2,1)}, bf16[10,32,896]{2,1,0:T(8,128)(2,1)}) custom-call(bf16[896,4096]{1,0:T(8,128)(2,1)} %fusion.6.a, bf16[896,4096]{1,0:T(8,128)(2,1)} %bitcast.78, bf16[5,896,512]{2,1,0:T(8,128)(2,1)} %get-tuple-element.31.wg, bf16[5,896,512]{2,1,0:T(8,128)(2,1)} %get-tuple-element.30.wu, ...), custom_call_target="tpu_custom_call" | custom-call | flops 150323855360 | bytes 22020096 | tf_op jit(solution)/shard_map/layer_backward_1/pallas_call | solution.py:223
  607.4 2.5 fusion.20
  609.9 8.3 fusion.7
  618.3 10.8 %add_convert_fusion.1.dh = bf16[896,4096]{1,0:T(8,128)(2,1)} fusion(bf16[896,4096]{1,0:T(8,128)(2,1)S(1)} %bitcast.77, bf16[896,4096]{1,0:T(8,128)(2,1)} %get-tuple-element.14, f32[4096]{0:T(1024)S(1)} %fusion.16, f32[4096]{0:T(1024)S(1)} %copy-done.11, bf16[1,4096,896]{1,2,0:T(8,128)(2,1)} %copy.16), kind=kLoop, calls=%fused_computation.24 | loop fusion | flops 36700160 | bytes 29392896 | tf_op jit(solution)/shard_map/convert_element_type | solution.py:370
  629.1 227.7 %layer_backward_0.1 = (bf16[896,4096]{1,0:T(8,128)(2,1)}, bf16[10,112,512]{2,1,0:T(8,128)(2,1)}, bf16[10,32,896]{2,1,0:T(8,128)(2,1)}) custom-call(bf16[896,4096]{1,0:T(8,128)(2,1)} %fusion.13.a, bf16[896,4096]{1,0:T(8,128)(2,1)} %add_convert_fusion.1.dh, bf16[5,896,512]{2,1,0:T(8,128)(2,1)} %get-tuple-element.33.wg, ...), custom_call_target="tpu_custom_call" | custom-call | flops 150323855360 | bytes 22020096 | tf_op jit(solution)/shard_map/layer_backward_0/pallas_call | solution.py:223
  856.8 2.4 pad_maximum_fusion.1
  859.2 1.5 fusion.19
  860.7 8.3 fusion.4
  869.1 10.8 %fusion.15 = bf16[1,4096,896]{1,2,0:T(8,128)(2,1)} fusion(bf16[896,4096]{1,0:T(8,128)(2,1)} %add_convert_fusion.1.dh, bf16[896,4096]{1,0:T(8,128)(2,1)} %get-tuple-element.15, bf16[1,4096,896]{1,2,0:T(8,128)(2,1)S(1)} %bitcast.75, f32[4096]{0:T(1024)S(1)} %fusion.17, f32[4096]{0:T(1024)S(1)} %copy-done.9), kind=kLoop, calls=%fused_computation.25 | loop fusion | flops 36700160 | bytes 29392896 | tf_op jit(solution)/shard_map/broadcast_in_dim | solution.py:396
  879.9 10.9 %copy.29 = bf16[1,4096,896]{2,1,0:T(8,128)(2,1)} copy(bf16[1,4096,896]{1,2,0:T(8,128)(2,1)} %fusion.15) | data formatting | bytes 14680064
  892.1 1.4 copy.31
  894.8 1.4 copy.30
  (42 shorter events, 2.9 us)
Async XLA Ops:
  21.0 5.9 copy-start
  25.7 0.6 copy-start.4
  26.4 0.6 copy-start.8
  243.3 15.4 %copy-start.1 = (bf16[2,5,8,64,896]{4,3,2,1,0:T(8,128)(2,1)S(1)}, bf16[2,5,8,64,896]{4,3,2,1,0:T(8,128)(2,1)}, u32[]{:S(2)}) copy-start(bf16[2,5,8,64,896]{4,3,2,1,0:T(8,128)(2,1)} %get-tuple-element.13) | copy-start | bytes 27525124
  369.1 0.6 copy-start.6
  369.8 0.6 copy-start.10
  607.4 10.8 %slice-start.2 = ((s8[7340032]{0:T(1024)(128)(4,1)}), s8[4194304]{0:T(1024)(128)(4,1)S(1)}, s32[]{:S(2)}) async-start(s8[7340032]{0:T(1024)(128)(4,1)} %bitcast.76), calls=%async_computation.2 | async-start | bytes 8388608
  609.9 8.4 copy-start.7
  609.9 8.4 slice-start.3
  609.9 8.4 copy-start.11
  859.2 9.9 %slice-start = ((s8[7340032]{0:T(1024)(128)(4,1)}), s8[4194304]{0:T(1024)(128)(4,1)S(1)}, s32[]{:S(2)}) async-start(s8[7340032]{0:T(1024)(128)(4,1)} %bitcast.74), calls=%async_computation | async-start | bytes 8388608
  860.7 8.4 copy-start.5
  860.7 8.4 slice-start.1
  860.7 8.4 copy-start.9
  879.9 11.2 %copy-start.3 = (bf16[10,112,256]{2,1,0:T(8,128)(2,1)S(1)}, bf16[10,112,256]{2,1,0:T(8,128)(2,1)}, u32[]{:S(2)}) copy-start(bf16[10,112,256]{2,1,0:T(8,128)(2,1)} %get-tuple-element.38) | copy-start | bytes 1720324
  890.8 3.0 copy-start.2

commit v2 on v1

v2 whole, which is shorter than its diff:
```python
import functools

import jax
import jax.numpy as jnp
from jax import lax
from jax.experimental import pallas as pl
from jax.experimental.pallas import tpu as pltpu
from jax.sharding import PartitionSpec as P

MESH = pl.DeviceIdType.MESH
F32, BF16 = jnp.float32, jnp.bfloat16
NC = 10
VMEM = 67_000_000
TILE = 1024
WIDE = 2048


def dot(a, b):
    return jnp.dot(a, b, preferred_element_type=F32)


def dot_nt(a, b):
    return lax.dot_general(a, b, (((1,), (1,)), ((), ())), preferred_element_type=F32)


def sigmoid(x):
    return 0.5 * jnp.tanh(0.5 * x) + 0.5


def scale_of(wide):
    return lax.rsqrt(jnp.mean(wide * wide, 0, keepdims=True) + 1e-6)


PIECES, STAGES, SPACE = NC, 5, 2
WAVES = PIECES + SPACE * STAGES


class Gather:
    def __init__(self, cols, rows, cols_all, rows_all, send, recv, local):
        self.refs = cols, rows, cols_all, rows_all
        self.sems = send, recv, local
        me, rep = lax.axis_index("dp"), lax.axis_index("rep")
        core, z0, z1 = me % 2, (me // 2) % 2, me // 4
        x, y = rep // 2, rep % 2
        self.me, self.rep = me, rep
        self.sibling, self.near, self.far = me + 1 - 2 * core, me + 2 - 4 * z0, me + 4 - 8 * z1
        self.others = self.far, self.near, self.far + 2 - 4 * z0
        self.by_x, self.by_y = rep + 2 - 4 * x, rep + 1 - 2 * y

    def greet(self):
        barrier = pltpu.get_barrier_semaphore()
        peers = [{"dp": self.far}, {"dp": self.near}, {"rep": self.by_x}, {"rep": self.by_y}, {"dp": self.sibling}]
        for p in peers:
            pl.semaphore_signal(barrier, 1, device_id=p, device_id_type=MESH)
        pl.semaphore_wait(barrier, len(peers))

    def place(self):
        cols, rows, cols_all, rows_all = self.refs
        return [pltpu.make_async_copy(cols, cols_all.at[:, :, self.me], self.sems[2].at[0]),
                pltpu.make_async_copy(rows, rows_all.at[:, self.me], self.sems[2].at[1])]

    def own(self, piece, quarter=None):
        cols, rows = self.refs[:2]
        i = piece // 2
        if piece % 2 == 0:
            q = cols.shape[-1] // 4
            return cols.at[:, i] if quarter is None else cols.at[:, i, :, pl.ds(pl.multiple_of(quarter * q, q), q)]
        r = rows.shape[-2] // 4
        return rows.at[i] if quarter is None else rows.at[i, pl.ds(pl.multiple_of(quarter * r, r), r), :]

    def part(self, piece, owner, quarter=None):
        cols, rows = self.refs[2:]
        i = piece // 2
        if piece % 2 == 0:
            q = cols.shape[-1] // 4
            if quarter is None:
                return cols.at[:, i, owner]
            return cols.at[:, i, owner, :, pl.ds(pl.multiple_of(quarter * q, q), q)]
        r = rows.shape[-2] // 4
        if quarter is None:
            return rows.at[i, owner]
        return rows.at[i, owner, pl.ds(pl.multiple_of(quarter * r, r), r), :]

    def copies(self, piece, s):
        me, rep = self.me, self.rep
        flip = (piece // 2 + piece) % 2
        one, two = (self.by_y, self.by_x) if flip else (self.by_x, self.by_y)
        far, near, _ = self.others
        if s == 0:
            moves = [(self.own(piece, rep), self.part(piece, me, rep), {"dp": far}, 0)]
        elif s == 1:
            moves = [(self.own(piece, rep), self.part(piece, me, rep), {"dp": near}, 1),
                     (self.part(piece, far, rep), self.part(piece, far, rep), {"dp": near}, 2)]
        elif s == 2:
            moves = [(self.part(piece, o, rep), self.part(piece, o, rep), {"rep": one}, 3 + n) for n, o in enumerate(self.others)]
        elif s == 3:
            moves = [(self.part(piece, o, w), self.part(piece, o, w), {"rep": two}, 6 + 2 * n + k)
                     for n, o in enumerate(self.others) for k, w in enumerate((rep, one))]
        else:
            moves = [(self.own(piece), self.part(piece, me), {"dp": self.sibling}, 12)]
            moves += [(self.part(piece, o), self.part(piece, o), {"dp": self.sibling}, 13 + n) for n, o in enumerate(self.others)]
        send, recv, _ = self.sems
        return [pltpu.make_async_remote_copy(src_ref=a, dst_ref=b, send_sem=send.at[piece, n], recv_sem=recv.at[piece, n],
                                             device_id=dev, device_id_type=MESH) for a, b, dev, n in moves]

    def wave(self, w):
        if w == 0:
            self.greet()
            for copy in self.place():
                copy.start()
        for s in reversed(range(STAGES + 1)):
            piece = w - SPACE * s
            if 0 <= piece < PIECES:
                if s:
                    for copy in self.copies(piece, s - 1):
                        copy.wait_recv()
                if s < STAGES:
                    for copy in self.copies(piece, s):
                        copy.start()
        if w == WAVES - 1:
            for piece in range(PIECES):
                for s in range(STAGES):
                    for copy in self.copies(piece, s):
                        copy.wait_send()
            for copy in self.place():
                copy.wait()


def gather_io(cols, rows):
    anywhere = pl.BlockSpec(memory_space=pl.ANY)
    inside = [pl.BlockSpec(t.shape, lambda s, n=t.ndim: (0,) * n, pipeline_mode=pl.Buffered(1)) for t in (cols, rows)]
    shapes = [jax.ShapeDtypeStruct((2, NC // 2, 8, *cols.shape[2:]), BF16), jax.ShapeDtypeStruct((NC // 2, 8, *rows.shape[1:]), BF16)]
    sems = [pltpu.SemaphoreType.DMA((PIECES, 16)), pltpu.SemaphoreType.DMA((PIECES, 16)), pltpu.SemaphoreType.DMA((2,))]
    return inside, [anywhere, anywhere], shapes, sems


FIRST = 16


def first_kernel(cols, rows, x, dy, cols_all, rows_all, h, a, by_y, send, recv, local):
    step = pl.program_id(0)
    gather = Gather(cols, rows, cols_all, rows_all, send, recv, local)
    for w in range(WAVES):
        pl.when(step == w)(functools.partial(gather.wave, w))

    @pl.when(step < FIRST)
    def _():
        turned = x[...].T
        h[...] = turned
        wide = turned.astype(F32)
        a[...] = (wide * scale_of(wide)).astype(BF16)
        by_y[...] = dy[...].T


def first(cols, rows, x, dy):
    tokens, d = x.shape
    size = tokens // FIRST
    inside, anywhere, shapes, sems = gather_io(cols, rows)
    tall = pl.BlockSpec((size, d), lambda s: (jnp.minimum(s, FIRST - 1), 0))
    wide = pl.BlockSpec((d, size), lambda s: (0, jnp.minimum(s, FIRST - 1)))
    state = jax.ShapeDtypeStruct((d, tokens), BF16)
    return pl.pallas_call(
        first_kernel,
        grid=(WAVES,),
        out_shape=[*shapes, state, state, state],
        in_specs=[*inside, tall, tall],
        out_specs=[*anywhere, wide, wide, wide],
        scratch_shapes=sems,
        compiler_params=pltpu.CompilerParams(collective_id=0, has_side_effects=True, vmem_limit_bytes=VMEM),
        cost_estimate=pl.CostEstimate(flops=10**11, bytes_accessed=6 * 10**7, transcendentals=0),
        name="gather_first",
    )(cols, rows, x, dy)


def forward_kernel(a, h, wg, wu, wd, cols, rows, h_out, a_out, cols_all, rows_all, acc, wgt, wut, wdt, send, recv, local):
    step = pl.program_id(0)
    c = wgt.shape[0]
    d, tokens = a.shape
    gather = Gather(cols, rows, cols_all, rows_all, send, recv, local)

    def waves(i):
        gather.wave(2 * i)
        gather.wave(2 * i + 1)

    for i in range(NC):
        pl.when(step == i)(functools.partial(waves, i))

    wgt[...] = wg[0, 0].T
    wut[...] = wu[0, 0].T
    wdt[...] = wd[0].reshape(c, d).T

    @pl.when(step == 0)
    def _():
        acc[...] = jnp.zeros_like(acc)

    def body(t, _):
        for k in range(2):
            at = pl.ds(pl.multiple_of((2 * t + k) * TILE, TILE), TILE)
            x = a[:, at]
            gate, up = dot(wgt[...], x), dot(wut[...], x)
            hid = (gate * sigmoid(gate) * up).astype(BF16)
            acc[:, at] += dot(wdt[...], hid)
        return 0

    lax.fori_loop(0, tokens // TILE // 2, body, 0)

    @pl.when(step == NC - 1)
    def _():
        def finish(t, _):
            at = pl.ds(pl.multiple_of(t * 256, 256), 256)
            out = (h[:, at].astype(F32) + acc[:, at].astype(BF16).astype(F32)).astype(BF16)
            h_out[:, at] = out
            wide = out.astype(F32)
            a_out[:, at] = (wide * scale_of(wide)).astype(BF16)
            return 0

        lax.fori_loop(0, tokens // 256, finish, 0)


def weight_specs(d, c):
    at = lambda s: jnp.minimum(s, NC - 1)
    gate = pl.BlockSpec((1, 1, d, c), lambda s: (0, at(s) // 2, 0, at(s) % 2))
    up = pl.BlockSpec((1, 1, d, c), lambda s: (1, at(s) // 2, 0, at(s) % 2))
    down = pl.BlockSpec((1, 8, c // 8, d), lambda s: (at(s) // 2, 0, at(s) % 2, 0))
    return [gate, up, down]


def forward(a, h, w, wd, cols, rows):
    d, tokens = a.shape
    c = w.shape[3] // 2
    whole = pl.BlockSpec((d, tokens), lambda s: (0, 0), pipeline_mode=pl.Buffered(1))
    state = jax.ShapeDtypeStruct((d, tokens), BF16)
    inside, anywhere, shapes, sems = gather_io(cols, rows)
    assert WAVES == 2 * NC
    return pl.pallas_call(
        forward_kernel,
        grid=(NC,),
        out_shape=[state, state, *shapes],
        in_specs=[whole, whole, *weight_specs(d, c), *inside],
        out_specs=[whole, whole, *anywhere],
        scratch_shapes=[
            pltpu.VMEM((d, tokens), F32),
            pltpu.VMEM((c, d), BF16),
            pltpu.VMEM((c, d), BF16),
            pltpu.VMEM((d, c), BF16),
            *sems,
        ],
        compiler_params=pltpu.CompilerParams(vmem_limit_bytes=VMEM, collective_id=3, has_side_effects=True),
        cost_estimate=pl.CostEstimate(flops=6 * d * tokens * c * NC, bytes_accessed=8 * d * tokens, transcendentals=0),
        name="layer_forward",
    )(a, h, w, w, wd, cols, rows)


def backward_kernel(a, dh, wg, wu, wd, h, out, gu_out, d_out,
                    acc, wt, wgu, hid, dgu, gu, dd,
                    sa_gu, sa_d, ra_gu, ra_d, ka_gu, ka_d,
                    sb_gu, sb_d, rb_gu, rb_d, kb_gu, kb_d,
                    sc_gu, sc_d, rc_gu, rc_d, o_gu, o_d,
                    send, recv, out_sem, h_sem):
    step = pl.program_id(0)
    me = lax.axis_index("dp")
    core, z0, z1 = me % 2, (me // 2) % 2, me // 4
    partners = (me + 1 - 2 * core, me + 2 - 4 * z0, me + 4 - 8 * z1)
    d, tokens = a.shape
    c = hid.shape[0]
    fetch = pltpu.make_async_copy(h, out, h_sem)

    @pl.when(step == 0)
    def _():
        fetch.start()
        barrier = pltpu.get_barrier_semaphore()
        for p in partners:
            pl.semaphore_signal(barrier, 1, device_id={"dp": p}, device_id_type=MESH)
        pl.semaphore_wait(barrier, 3)
        acc[...] = jnp.zeros_like(acc)

    def copies(stage, slot):
        pairs = (((sa_gu, ra_gu), (sa_d, ra_d)), ((sb_gu, rb_gu), (sb_d, rb_d)), ((sc_gu, rc_gu), (sc_d, rc_d)))[stage]
        return [
            pltpu.make_async_remote_copy(
                src_ref=s, dst_ref=r.at[slot], send_sem=send.at[stage, n], recv_sem=recv.at[stage, n, slot],
                device_id={"dp": partners[stage]}, device_id_type=MESH)
            for n, (s, r) in enumerate(pairs)
        ]

    def outs(chunk):
        return [pltpu.make_async_copy(o_gu, gu_out.at[chunk], out_sem.at[0]),
                pltpu.make_async_copy(o_d, d_out.at[chunk], out_sem.at[1])]

    @pl.when(step < NC)
    def _():
        wt[:c] = wg[0, 0].T
        wt[c:] = wu[0, 0].T
        wgu[:, :c] = wg[0, 0]
        wgu[:, c:] = wu[0, 0]

        def body(t, _):
            for k in range(2):
                at = pl.ds(pl.multiple_of((2 * t + k) * TILE, TILE), TILE)
                x = a[:, at]
                gate, up = dot(wt[:c], x), dot(wt[c:], x)
                by_hid = dot(wd[0].reshape(c, d), dh[:, at]).astype(BF16).astype(F32)
                sig = sigmoid(gate)
                silu = gate * sig
                hid[:, at] = (silu * up).astype(BF16)
                dgu[:c, at] = (by_hid * up * (sig + silu * (1.0 - sig))).astype(BF16)
                dgu[c:, at] = (by_hid * silu).astype(BF16)
            return 0

        lax.fori_loop(0, tokens // TILE // 2, body, 0)

    @pl.when(step == NC)
    def _():
        fetch.wait()

        def finish(t, _):
            at = pl.ds(pl.multiple_of(t * 256, 256), 256)
            wide, g = out[:, at].astype(F32), acc[:, at].astype(BF16).astype(F32)
            scale = scale_of(wide)
            through = g * scale - wide * (scale**3 * jnp.mean(g * wide, 0, keepdims=True))
            out[:, at] = (dh[:, at].astype(F32) + through.astype(BF16).astype(F32)).astype(BF16)
            return 0

        lax.fori_loop(0, tokens // 256, finish, 0)

    @pl.when(step >= 4)
    def _():
        for copy in outs(step - 4):
            copy.wait()

    @pl.when(step >= 3)
    def _():
        slot = (step - 3) % 2
        for copy in copies(2, slot):
            copy.wait()
        o_gu[...] = (kb_gu[z1] + rc_gu[slot].astype(F32)).astype(BF16)
        o_d[...] = (kb_d[z1] + rc_d[slot].astype(F32)).astype(BF16)
        for copy in outs(step - 3):
            copy.start()

    @pl.when((step >= 2) & (step < NC + 2))
    def _():
        slot = (step - 2) % 2
        for copy in copies(1, slot):
            copy.wait()
        for half in range(2):
            kb_gu[half] = ka_gu[half, z0] + rb_gu[slot, half].astype(F32)
            kb_d[half] = ka_d[half, z0] + rb_d[slot, half].astype(F32)
        sc_gu[...] = kb_gu[1 - z1].astype(BF16)
        sc_d[...] = kb_d[1 - z1].astype(BF16)
        for copy in copies(2, slot):
            copy.start()

    @pl.when((step >= 1) & (step < NC + 1))
    def _():
        slot = (step - 1) % 2
        for copy in copies(0, slot):
            copy.wait()
        for i in range(2):
            for j in range(2):
                ka_gu[i, j] = gu[i, j, core] + ra_gu[slot, i, j].astype(F32)
                ka_d[i, j] = dd[i, j, core] + ra_d[slot, i, j].astype(F32)
            sb_gu[i] = ka_gu[i, 1 - z0].astype(BF16)
            sb_d[i] = ka_d[i, 1 - z0].astype(BF16)
        for copy in copies(1, slot):
            copy.start()

    @pl.when(step < NC)
    def _():
        def body(t, _):
            at = pl.ds(pl.multiple_of(t * WIDE, WIDE), WIDE)
            g = dgu[:, at]
            acc[:, at] += dot(wgu[...], g)
            return 0

        lax.fori_loop(0, tokens // WIDE, body, 0)

        shape = gu.shape
        gu[...] = dot_nt(a[...], dgu[...]).reshape(shape)
        dd[...] = dot_nt(dh[...], hid[...]).T.reshape(dd.shape)
        for i in range(2):
            for j in range(2):
                sa_gu[i, j] = gu[i, j, 1 - core].astype(BF16)
                sa_d[i, j] = dd[i, j, 1 - core].astype(BF16)
        for copy in copies(0, step % 2):
            copy.start()

    @pl.when(step == NC + 2)
    def _():
        for copy in outs(NC - 1):
            copy.wait()


def backward(a, dh, h, w, wd, number):
    d, tokens = a.shape
    c = w.shape[3] // 2
    m, n = d // 8, c // 8
    whole = pl.BlockSpec((d, tokens), lambda s: (0, 0), pipeline_mode=pl.Buffered(1))
    anywhere = pl.BlockSpec(memory_space=pl.ANY)
    both = lambda *lead, dtype: [pltpu.VMEM((*lead, m, 2 * c), dtype), pltpu.VMEM((*lead, n, d), dtype)]
    return pl.pallas_call(
        backward_kernel,
        grid=(NC + 3,),
        out_shape=[
            jax.ShapeDtypeStruct((d, tokens), BF16),
            jax.ShapeDtypeStruct((NC, m, 2 * c), BF16),
            jax.ShapeDtypeStruct((NC, n, d), BF16),
        ],
        in_specs=[whole, whole, *weight_specs(d, c), anywhere],
        out_specs=[whole, anywhere, anywhere],
        scratch_shapes=[
            pltpu.VMEM((d, tokens), F32),
            pltpu.VMEM((2 * c, d), BF16),
            pltpu.VMEM((d, 2 * c), BF16),
            pltpu.VMEM((c, tokens), BF16),
            pltpu.VMEM((2 * c, tokens), BF16),
            *both(2, 2, 2, dtype=F32),
            *both(2, 2, dtype=BF16), *both(2, 2, 2, dtype=BF16), *both(2, 2, dtype=F32),
            *both(2, dtype=BF16), *both(2, 2, dtype=BF16), *both(2, dtype=F32),
            *both(dtype=BF16), *both(2, dtype=BF16), *both(dtype=BF16),
            pltpu.SemaphoreType.DMA((3, 2)),
            pltpu.SemaphoreType.DMA((3, 2, 2)),
            pltpu.SemaphoreType.DMA((2,)),
            pltpu.SemaphoreType.DMA,
        ],
        compiler_params=pltpu.CompilerParams(vmem_limit_bytes=VMEM, collective_id=1 + number, has_side_effects=True),
        cost_estimate=pl.CostEstimate(flops=16 * d * tokens * c * NC, bytes_accessed=6 * d * tokens, transcendentals=0),
        name=f"layer_backward_{number}",
    )(a, dh, w, w, wd, h)


def solution(mesh):
    def local(x, dy, wg, wu, wd):
        layers, m, ff = wg.shape
        d = wd.shape[2]
        n = wd.shape[1] // NC

        def ordered(w):
            w = w.reshape(layers, m, 8, NC // 2, 2, n).transpose(0, 3, 1, 4, 2, 5)
            return w.reshape(layers, NC // 2, m, 16 * n)

        cols = jnp.stack([ordered(wg), ordered(wu)], 1)
        rows = wd.reshape(layers, NC // 2, 2 * n, d)
        together = lambda w: w.reshape(2, NC // 2, d, 16 * n)
        w0, wd0, h0, a0, by_y = first(cols[0], rows[0], x[0], dy[0])
        w0 = together(w0)
        h1, a1, w1, wd1 = forward(a0, h0, w0, wd0, cols[1], rows[1])
        by_h1, gu1, d1 = backward(a1, by_y, h1, together(w1), wd1, 1)
        by_h0, gu0, d0 = backward(a0, by_h1, h0, w0, wd0, 0)
        by_x = by_h0.T[None]

        def restored(*both):
            w = jnp.stack(both).reshape(layers, NC, m, 8, n).transpose(0, 2, 3, 1, 4)
            return w.reshape(layers, m, ff)

        half = 8 * n
        return (by_x, restored(gu0[..., :half], gu1[..., :half]), restored(gu0[..., half:], gu1[..., half:]),
                jnp.stack([d0, d1]).reshape(layers, NC * n, d))

    seq = P(("rep", "dp"), None, None)
    w = P(None, "dp", None)
    g = P("rep", "dp", None)
    return jax.shard_map(local, mesh=mesh, in_specs=(seq, seq, w, w, w), out_specs=(seq, g, g, g), check_vma=False)
```

time: 904 us -> 698 us (0.77)
  Pallas kernels: 750 us -> 657 us
  other arithmetic: 73.9 us -> 4.53 us
  local copies, waits for them, and re-layouts: 71.3 us -> 26.2 us
    pallas_call x2, Pallas kernels: 294 us -> 201 us  [the longest x1 116 us: forward(): pl.pallas_call(forward_kernel, grid=(NC,), out_shape=[state, state, *shap...]
    reduce_sum x4 -> x0, other arithmetic: 33.7 us -> none  [the longest x2 17 us: scale_of(): return lax.rsqrt(jnp.mean(wide ** 2, 0, keepdims=True) + 1e-06)]
    unnamed x39 -> x15, local copies, waits for them, and re-layouts: 42.1 us -> 17 us
    convert_element_type x3 -> x0, other arithmetic: 24.5 us -> none  [the longest x2 13.7 us: normed(): return (h.astype(F32) * scale_of(h)).astype(BF16)]
    squeeze x2 -> x0, local copies, waits for them, and re-layouts: 19.2 us -> none  [local(): weights = [(cols[i, 0], cols[i, 1], rows[i]) for i in range(layers)]]
    broadcast_in_dim x1 -> x0, other arithmetic: 10.8 us -> none  [local(): by_x = through_norm(h0, by_a0, by_h1).T[None]]
where the time goes in v2:
time: 698 us; the launch traced here: 689 us
  Pallas kernels  657 us (94%)
  local copies, waits for them, and re-layouts  26.2 us (4%)
    pallas_call x2, Pallas kernels, backward(): pl.pallas_call(backward_kernel, grid=(NC + 3,), out_shape=[jax.ShapeDtype...  456 us
    pallas_call x1, Pallas kernels, forward(): pl.pallas_call(forward_kernel, grid=(NC,), out_shape=[state, state, *shap...  116 us
    pallas_call x1, Pallas kernels, first(): pl.pallas_call(first_kernel, grid=(WAVES,), out_shape=[*shapes, state, st...  84.9 us
    unnamed x15, local copies, waits for them, and re-layouts  17 us

profile of v2, /device:TPU:0, one launch (start us, length us, event | category | flops | bytes accessed | tf_op | source)
XLA Modules:
  0.0 689.1 jit_solution(6206640780445260918)
XLA Ops:
  0.6 2.4 fusion.5
  3.1 0.8 copy.14
  3.9 0.3 copy.15
  4.2 1.4 copy.18
  5.6 1.7 copy.16
  7.3 0.3 copy.17
  7.6 0.0 copy-start
  7.6 1.4 copy.19
  9.1 2.8 fusion.2
  11.9 84.9 %gather_first.1 = (bf16[2,5,8,112,512]{4,3,2,1,0:T(8,128)(2,1)}, bf16[5,8,64,896]{3,2,1,0:T(8,128)(2,1)}, bf16[896,4096]{1,0:T(8,128)(2,1)}, bf16[896,4096]{1,0:T(8,128)(2,1)}, bf16[896,4096]{1,0:T(8,128)(2,1)}) custom-call(bf16[2,5,112,512]{3,2,1,0:T(8,128)(2,1)} %get-tuple-element.43.cols, bf16[5,64,896]{2,1,0:T(8,128)(2,1)} %bitcast.45, ...), custom_call_target="tpu_custom_call" | custom-call | flops 99999997952 | bytes 60000000 | tf_op jit(solution)/shard_map/gather_first/pallas_call | solution.py:162
  96.7 115.9 %layer_forward.1 = (bf16[896,4096]{1,0:T(8,128)(2,1)}, bf16[896,4096]{1,0:T(8,128)(2,1)}, bf16[2,5,8,112,512]{4,3,2,1,0:T(8,128)(2,1)}, bf16[5,8,64,896]{3,2,1,0:T(8,128)(2,1)}) custom-call(bf16[896,4096]{1,0:T(8,128)(2,1)} %get-tuple-element.19.a, bf16[896,4096]{1,0:T(8,128)(2,1)} %get-tuple-element.20.h, bf16[2,5,896,512]{3,2,1,0:T(8,128)(2,1)} %bitcast.50, ...), custom_call_target="tpu_custom_call" | custom-call | flops 56371445760 | bytes 29360128 | tf_op jit(solution)/shard_map/layer_forward/pallas_call | solution.py:235
  212.7 228.0 %layer_backward_1.1 = (bf16[896,4096]{1,0:T(8,128)(2,1)}, bf16[10,112,512]{2,1,0:T(8,128)(2,1)}, bf16[10,32,896]{2,1,0:T(8,128)(2,1)}) custom-call(bf16[896,4096]{1,0:T(8,128)(2,1)} %get-tuple-element.23.a, bf16[896,4096]{1,0:T(8,128)(2,1)} %get-tuple-element.24.dh, bf16[2,5,896,512]{3,2,1,0:T(8,128)(2,1)} %bitcast.54, bf16[2,5,896,512]{3,2,1,0:T(8,128)(2,1)} %bitcast.55, ...), custom_call_target="tpu_custom_call" | custom-call | flops 150323855360 | bytes 22020096 | tf_op jit(solution)/shard_map/layer_backward_1/pallas_call | solution.py:401
  440.6 228.3 %layer_backward_0.1 = (bf16[896,4096]{1,0:T(8,128)(2,1)}, bf16[10,112,512]{2,1,0:T(8,128)(2,1)}, bf16[10,32,896]{2,1,0:T(8,128)(2,1)}) custom-call(bf16[896,4096]{1,0:T(8,128)(2,1)} %get-tuple-element.19.a, bf16[896,4096]{1,0:T(8,128)(2,1)} %get-tuple-element.28.dh, bf16[2,5,896,512]{3,2,1,0:T(8,128)(2,1)} %bitcast.52, bf16[2,5,896,512]{3,2,1,0:T(8,128)(2,1)} %bitcast.53, ...), custom_call_target="tpu_custom_call" | custom-call | flops 150323855360 | bytes 22020096 | tf_op jit(solution)/shard_map/layer_backward_0/pallas_call | solution.py:401
  669.0 0.0 copy-start.3
  669.0 0.0 copy-start.4
  669.0 11.1 %copy.26 = bf16[1,4096,896]{2,1,0:T(8,128)(2,1)} copy(bf16[1,4096,896]{1,2,0:T(8,128)(2,1)} %bitcast.33) | data formatting | bytes 14680064
  680.2 0.0 copy-done.3
  680.2 0.0 copy-done.4
  680.2 1.1 pad_maximum_fusion.1
  681.3 0.5 copy-done.2
  681.8 0.1 fusion.3
  681.9 0.3 copy.23
  682.3 0.3 copy.20
  682.6 1.3 fusion.4
  683.9 0.3 copy.24
  684.2 0.3 maximum_bitcast_fusion.1
  684.5 0.3 copy.25
  684.9 1.4 copy.28
  686.3 0.3 copy.21
  686.6 0.3 maximum_bitcast_fusion
  686.9 0.3 copy.22
  687.3 1.4 copy.27
  (4 shorter events, 0.0 us)
Async XLA Ops:
  0.6 2.4 copy-start.1
  7.6 1.4 copy-start
  669.0 11.2 %copy-start.3 = (bf16[10,32,896]{2,1,0:T(8,128)(2,1)S(1)}, bf16[10,32,896]{2,1,0:T(8,128)(2,1)}, u32[]{:S(2)}) copy-start(bf16[10,32,896]{2,1,0:T(8,128)(2,1)} %get-tuple-element.33) | copy-start | bytes 1720324
  669.0 11.2 %copy-start.4 = (bf16[10,32,896]{2,1,0:T(8,128)(2,1)S(1)}, bf16[10,32,896]{2,1,0:T(8,128)(2,1)}, u32[]{:S(2)}) copy-start(bf16[10,32,896]{2,1,0:T(8,128)(2,1)} %get-tuple-element.32) | copy-start | bytes 1720324
  680.2 1.7 copy-start.2
